TPU v7x, 16 devices: a 4x2x1 block of a 4x4x8 slice. The times are simulated.
16 devices in a mesh: dp: 2 (over y, z), tp: 8 (over x, core).
Axes of the slice: x: 4, y: 2, z: 1, core: 2. Of those that a mesh axis runs over, the one named last changes fastest.
The devices are a block of a 4x4x8 slice.
Arguments:
- tokens: bfloat16 [4, 1024, 4096], P('dp', 'tp'), parts along dimension 0
- pad_mask: int32 [4, 1024], P('dp'), parts along dimension 0
- rel_table: float32 [32, 64], P(None, 'tp')
- w_query: bfloat16 [2, 4096, 4096], P(None, None, 'tp')
- w_key: bfloat16 [2, 4096, 4096], P(None, None, 'tp')
- w_value: bfloat16 [2, 4096, 4096], P(None, None, 'tp')
- w_out: bfloat16 [2, 4096, 4096], P(None, 'tp')
- w_act: bfloat16 [2, 4096, 10240], P(None, None, 'tp')
- w_lin: bfloat16 [2, 4096, 10240], P(None, None, 'tp')
- w_down: bfloat16 [2, 10240, 4096], P(None, 'tp')
- norm_attn: float32 [2, 4096], replicated
- norm_mlp: float32 [2, 4096], replicated
Outputs:
- output: bfloat16 [4, 1024, 4096], P('dp', 'tp'), parts along dimension 0
There are 2 independent parts. A program takes and returns all parts, laid end to end along the dimension named above; an argument that names none is the same for every part.
All inputs are finite; a program needn't handle non-finite values.
Results may differ from a plain program's by a relative error of at most 0.02.
Values are sent between devices in bfloat16 or wider.
A program may use at most 768 MiB of HBM per device.

v0:
```python
import jax
import jax.numpy as jnp
from jax import lax
from jax.sharding import PartitionSpec as P


def rel_bucket(offsets):
    side = jnp.where(offsets > 0, 16, 0)
    distance = jnp.minimum(jnp.abs(offsets), 128)
    limits = 64 * 2 ** jnp.arange(1, 8)
    steps = jnp.sum((distance[:, None] * distance[:, None] >= limits[None, :]).astype(jnp.int32), axis=1)
    return side + jnp.where(distance < 8, distance, 8 + steps)


def rms_norm(rows_in, gain_vec):
    rows32 = rows_in.astype(jnp.float32)
    inv_rms = lax.rsqrt(jnp.mean(rows32 * rows32, axis=-1, keepdims=True) + 1e-6)
    return (rows32 * inv_rms * gain_vec).astype(jnp.bfloat16)


def bias_rows(dist_table, seq_len, row_start, row_count):
    padded = jnp.pad(dist_table, ((0, 0), (0, 1)))
    doubled = jnp.concatenate([padded, padded], axis=1)
    shifted = lax.dynamic_slice_in_dim(doubled, 2 * seq_len - row_start, 2 * seq_len, axis=1)
    tiled = jnp.tile(shifted, (1, row_count))[:, : row_count * (2 * seq_len - 1)]
    return tiled.reshape(dist_table.shape[0], row_count, 2 * seq_len - 1)[:, :, seq_len - 1:]


def solution(mesh):
    group_size = mesh.shape['tp']
    col_spec = P(None, None, 'tp')
    row_spec = P(None, 'tp', None)

    def local_fn(tokens, pad_mask, rel_table, w_query, w_key, w_value, w_out, w_act, w_lin, w_down, norm_attn, norm_mlp):
        batch, seq_loc, model_dim = tokens.shape
        seq_len = seq_loc * group_size
        head_count = rel_table.shape[1]
        head_dim = w_query.shape[2] // head_count
        offsets = jnp.arange(2 * seq_len - 1) - (seq_len - 1)
        rel_bias = bias_rows(jnp.take(rel_table.T, rel_bucket(offsets), axis=1), seq_len, 0, seq_len)
        key_bias = jnp.where(pad_mask == 1, 0.0, -1e9).astype(jnp.float32)[:, None, None, :]

        def project(gathered, weight_mat):
            projected = jnp.einsum('bsd,dn->bsn', gathered, weight_mat, preferred_element_type=jnp.float32)
            return projected.astype(jnp.bfloat16).reshape(batch, seq_len, head_count, head_dim)

        residual = tokens
        for layer_idx in range(w_query.shape[0]):
            gathered = lax.all_gather(rms_norm(residual, norm_attn[layer_idx]), 'tp', axis=1, tiled=True)
            query_proj = project(gathered, w_query[layer_idx])
            key_proj = project(gathered, w_key[layer_idx])
            value_proj = project(gathered, w_value[layer_idx])
            scores = jnp.einsum('bqhe,bkhe->bhqk', query_proj, key_proj, preferred_element_type=jnp.float32)
            attn_probs = jax.nn.softmax(scores + rel_bias + key_bias, axis=-1).astype(jnp.bfloat16)
            context = jnp.einsum('bhqk,bkhe->bqhe', attn_probs, value_proj, preferred_element_type=jnp.float32).astype(jnp.bfloat16)
            out_mat = w_out[layer_idx].reshape(head_count, head_dim, model_dim)
            part_out = jnp.einsum('crif,ife->cre', context, out_mat, preferred_element_type=jnp.float32).astype(jnp.bfloat16)
            attn_out = lax.psum_scatter(part_out, 'tp', scatter_dimension=1, tiled=True)
            mid_resid = (residual.astype(jnp.float32) + attn_out.astype(jnp.float32)).astype(jnp.bfloat16)
            gathered = lax.all_gather(rms_norm(mid_resid, norm_mlp[layer_idx]), 'tp', axis=1, tiled=True)
            act_proj = jnp.einsum('bsd,df->bsf', gathered, w_act[layer_idx], preferred_element_type=jnp.float32)
            lin_proj = jnp.einsum('bsd,df->bsf', gathered, w_lin[layer_idx], preferred_element_type=jnp.float32)
            gated = (jax.nn.gelu(act_proj, approximate=True) * lin_proj).astype(jnp.bfloat16)
            part_out = jnp.einsum('bsf,fd->bsd', gated, w_down[layer_idx], preferred_element_type=jnp.float32).astype(jnp.bfloat16)
            ffn_out = lax.psum_scatter(part_out, 'tp', scatter_dimension=1, tiled=True)
            residual = (mid_resid.astype(jnp.float32) + ffn_out.astype(jnp.float32)).astype(jnp.bfloat16)
        return residual

    in_specs = (P('dp', 'tp', None), P('dp', None), P(None, 'tp'), col_spec, col_spec, col_spec, row_spec,
                col_spec, col_spec, row_spec, P(None, None), P(None, None))
    return jax.shard_map(local_fn, mesh=mesh, in_specs=in_specs, out_specs=P('dp', 'tp', None), check_vma=False)
```

profile of v0, /device:TPU:112, one launch (start us, length us, event | category | flops | bytes accessed | tf_op | source)
XLA Modules:
  0.0 1503.7 jit_solution(1580777591696166000)
XLA Ops:
  6.6 1.5 fusion.109
  8.0 2.1 fusion.46
  10.1 3.5 fusion.48
  13.7 0.1 all-gather.5.cloned.1.call-update
  13.7 0.1 reduce-scatter.5.cloned.1.call-start
  13.8 0.1 copy.33
  13.9 0.1 convert_reduce_fusion
  14.0 5.5 gather_fusion
  19.5 0.3 select_bitcast_fusion
  19.9 0.3 copy.51
  20.2 21.3 %tile.4 = f32[8,1024,2048]{2,0,1:T(8,128)} broadcast(f32[8,2048]{1,0:T(8,128)S(1)} %pad.4.clone), dimensions={0,2} | broadcast | bytes 67174400 | tf_op jit(solution)/shard_map/tile | solution.py:25
  41.5 44.4 %slice.82 = f32[8,2096128]{1,0:T(8,128)} slice(f32[8,2097152]{1,0:T(8,128)} %bitcast.14), slice={[0:8], [0:2096128]} | slice | bytes 134152192 | tf_op jit(solution)/shard_map/slice | solution.py:25
  85.9 213.5 %reshape.186 = f32[16769024]{0:T(1024)} reshape(f32[8,2096128]{1,0:T(8,128)} %slice.82) | data formatting | bytes 134152192
  299.5 98.6 %reshape.158 = f32[8,1024,2047]{2,1,0:T(8,128)} reshape(f32[16769024]{0:T(1024)} %reshape.186) | data formatting | bytes 134152192 | tf_op jit(solution)/shard_map/reshape | solution.py:26
  398.0 26.4 %slice.83 = f32[8,1024,1024]{2,1,0:T(8,128)} slice(f32[8,1024,2047]{2,1,0:T(8,128)} %reshape.158), slice={[0:8], [0:1024], [1023:2047]} | slice | bytes 67108864 | tf_op jit(solution)/shard_map/slice | solution.py:26
  424.5 31.9 %copy.35 = f32[8,1024,1024]{1,2,0:T(8,128)} copy(f32[8,1024,1024]{2,1,0:T(8,128)} %slice.83) | data formatting | bytes 67108864 | tf_op jit(solution)/shard_map/slice | solution.py:26
  456.4 6.0 fusion.108
  462.3 13.7 fusion.87
  476.0 14.6 fusion.90
  490.7 40.8 %fusion.111 = (f32[2,8,1024]{2,1,0:T(8,128)S(1)}, f32[2,8,1024,1024]{2,3,1,0:T(8,128)}) fusion(f32[2,1024]{1,0:T(2,128)S(1)} %compare_select_fusion.5, f32[8,1024,1024]{1,2,0:T(8,128)} %copy.35, bf16[2,1024,8,64]{1,3,2,0:T(8,128)(2,1)S(1)} %bitcast.151, bf16[2,1024,8,64]{1,3,2,0:T(8,128)(2,1)} %bitcast.152), kind=kOutput, calls=%fused_computation.142 | convolution fusion | flops 2214593536 | bytes 104931328 | tf_op jit(solution)/shard_map/sub | solution.py:54
  531.4 13.7 fusion.84
  545.1 23.7 %fusion.154 = bf16[2,1024,8,64]{1,3,2,0:T(8,128)(2,1)} fusion(f32[2,8,1024,1024]{2,3,1,0:T(8,128)} %get-tuple-element.14, f32[2,8,1024]{2,1,0:T(8,128)S(1)} %get-tuple-element.13, bf16[2,1024,8,64]{1,3,2,0:T(8,128)(2,1)S(1)} %bitcast.161), kind=kOutput, calls=%fused_computation.102.clone | convolution fusion | flops 2181038080 | bytes 71368704 | tf_op jit(solution)/shard_map/bhqk,bkhe->bqhe/dot_general | solution.py:55
  568.9 14.3 bitcast_convert_fusion.1
  583.1 0.1 reduce-scatter.5.cloned.1.call-update
  583.2 0.1 all-gather.7.cloned.1.call-start
  583.3 0.6 copy-done.11
  583.9 0.6 fusion.110
  584.5 89.4 %reduce-scatter.5.cloned.1.call-done = bf16[2,128,4096]{2,1,0:T(8,128)(2,1)} async-done(((bf16[2,1024,4096]{2,1,0:T(8,128)(2,1)}), bf16[2,128,4096]{2,1,0:T(8,128)(2,1)}) %reduce-scatter.5.cloned.1.call-update) | async-done | bytes 2097168 | tf_op jit(solution)/shard_map/reduce_scatter | solution.py:58
  674.0 2.5 fusion.50
  676.5 2.4 fusion.52
  678.8 0.1 all-gather.7.cloned.1.call-update
  678.9 0.1 reduce-scatter.7.cloned.1.call-start
  679.0 80.8 %all-gather.7.cloned.1.call-done = bf16[2,1024,4096]{2,1,0:T(8,128)(2,1)} async-done(((bf16[2,128,4096]{2,1,0:T(8,128)(2,1)}), bf16[2,1024,4096]{2,1,0:T(8,128)(2,1)}) %all-gather.7.cloned.1.call-update) | async-done | bytes 16777232 | tf_op jit(solution)/shard_map/all_gather | solution.py:60
  759.8 26.5 %fusion.29 = f32[2,1024,1280]{2,1,0:T(8,128)S(1)} fusion(bf16[2,1024,4096]{2,1,0:T(8,128)(2,1)} %all-gather.7.cloned.1.call-done, bf16[2,4096,1280]{2,1,0:T(8,128)(2,1)} %param.20), kind=kOutput, calls=%fused_computation.42 | convolution fusion | flops 21474836480 | bytes 37748736 | tf_op jit(solution)/shard_map/bsd,df->bsf/dot_general | solution.py:62
  786.3 30.4 %multiply_convert_fusion.1 = bf16[2,1024,1280]{2,1,0:T(8,128)(2,1)} fusion(f32[2,1024,1280]{2,1,0:T(8,128)S(1)} %fusion.29, bf16[2,1024,4096]{2,1,0:T(8,128)(2,1)} %all-gather.7.cloned.1.call-done, bf16[2,4096,1280]{2,1,0:T(8,128)(2,1)} %param.19), kind=kOutput, calls=%fused_computation.50 | convolution fusion | flops 21501050880 | bytes 42991616 | tf_op jit(solution)/shard_map/bsd,df->bsf/dot_general | solution.py:61
  816.7 29.2 %convolution_convert_fusion.1 = bf16[2,1024,4096]{2,1,0:T(8,128)(2,1)} fusion(bf16[2,1024,1280]{2,1,0:T(8,128)(2,1)} %multiply_convert_fusion.1, bf16[2,1280,4096]{2,1,0:T(8,128)(2,1)} %param.21), kind=kOutput, calls=%fused_computation.22 | convolution fusion | flops 21483225088 | bytes 32505856 | tf_op jit(solution)/shard_map/bsf,fd->bsd/dot_general | solution.py:64
  845.9 0.1 reduce-scatter.7.cloned.1.call-update
  846.0 0.1 all-gather.9.cloned.1.call-start
  846.0 88.3 %reduce-scatter.7.cloned.1.call-done = bf16[2,128,4096]{2,1,0:T(8,128)(2,1)} async-done(((bf16[2,1024,4096]{2,1,0:T(8,128)(2,1)}), bf16[2,128,4096]{2,1,0:T(8,128)(2,1)}) %reduce-scatter.7.cloned.1.call-update) | async-done | bytes 2097168 | tf_op jit(solution)/shard_map/reduce_scatter | solution.py:65
  934.4 3.5 fusion.54
  937.9 1.3 copy-done.1
  939.2 2.1 fusion.56
  941.2 0.1 all-gather.9.cloned.1.call-update
  941.3 0.1 reduce-scatter.9.cloned.1.call-start
  941.3 80.8 %all-gather.9.cloned.1.call-done = bf16[2,1024,4096]{2,1,0:T(8,128)(2,1)} async-done(((bf16[2,128,4096]{2,1,0:T(8,128)(2,1)}), bf16[2,1024,4096]{2,1,0:T(8,128)(2,1)}) %all-gather.9.cloned.1.call-update) | async-done | bytes 16777232 | tf_op jit(solution)/shard_map/all_gather | solution.py:49
  1022.2 13.8 fusion.96
  1036.0 14.6 fusion.99
  1050.7 40.8 %fusion.112 = (f32[2,8,1024]{2,1,0:T(8,128)S(1)}, f32[2,8,1024,1024]{2,3,1,0:T(8,128)}) fusion(f32[2,1024]{1,0:T(2,128)S(1)} %copy-done.8, f32[8,1024,1024]{1,2,0:T(8,128)} %copy.35, bf16[2,1024,8,64]{1,3,2,0:T(8,128)(2,1)S(1)} %bitcast.149, bf16[2,1024,8,64]{1,3,2,0:T(8,128)(2,1)} %bitcast.150), kind=kOutput, calls=%fused_computation.143 | convolution fusion | flops 2214593536 | bytes 104931328 | tf_op jit(solution)/shard_map/sub | solution.py:54
  1091.5 13.7 fusion.93
  1105.2 23.7 %fusion.151 = bf16[2,1024,8,64]{1,3,2,0:T(8,128)(2,1)} fusion(f32[2,8,1024,1024]{2,3,1,0:T(8,128)} %get-tuple-element.16, f32[2,8,1024]{2,1,0:T(8,128)S(1)} %get-tuple-element.15, bf16[2,1024,8,64]{1,3,2,0:T(8,128)(2,1)S(1)} %bitcast.162), kind=kOutput, calls=%fused_computation.101.clone.1 | convolution fusion | flops 2181038080 | bytes 71368704 | tf_op jit(solution)/shard_map/bhqk,bkhe->bqhe/dot_general | solution.py:55
  1128.9 14.2 bitcast_convert_fusion
  1143.1 0.1 reduce-scatter.9.cloned.1.call-update
  1143.2 0.1 all-gather.11.cloned.1.call-start
  1143.3 88.4 %reduce-scatter.9.cloned.1.call-done = bf16[2,128,4096]{2,1,0:T(8,128)(2,1)} async-done(((bf16[2,1024,4096]{2,1,0:T(8,128)(2,1)}), bf16[2,128,4096]{2,1,0:T(8,128)(2,1)}) %reduce-scatter.9.cloned.1.call-update) | async-done | bytes 2097168 | tf_op jit(solution)/shard_map/reduce_scatter | solution.py:58
  1231.6 2.5 fusion.58
  1234.2 2.4 fusion.60
  1236.5 0.1 all-gather.11.cloned.1.call-update
  1236.6 0.1 reduce-scatter.11.cloned.1.call-start
  1236.7 80.8 %all-gather.11.cloned.1.call-done = bf16[2,1024,4096]{2,1,0:T(8,128)(2,1)} async-done(((bf16[2,128,4096]{2,1,0:T(8,128)(2,1)}), bf16[2,1024,4096]{2,1,0:T(8,128)(2,1)}) %all-gather.11.cloned.1.call-update) | async-done | bytes 16777232 | tf_op jit(solution)/shard_map/all_gather | solution.py:60
  1317.5 26.7 %fusion.25 = f32[2,1024,1280]{2,1,0:T(8,128)S(1)} fusion(bf16[2,1024,4096]{2,1,0:T(8,128)(2,1)} %all-gather.11.cloned.1.call-done, bf16[2,4096,1280]{2,1,0:T(8,128)(2,1)} %param.20), kind=kOutput, calls=%fused_computation.38 | convolution fusion | flops 21474836480 | bytes 37748736 | tf_op jit(solution)/shard_map/bsd,df->bsf/dot_general | solution.py:62
  1344.2 30.4 %multiply_convert_fusion = bf16[2,1024,1280]{2,1,0:T(8,128)(2,1)} fusion(f32[2,1024,1280]{2,1,0:T(8,128)S(1)} %fusion.25, bf16[2,1024,4096]{2,1,0:T(8,128)(2,1)} %all-gather.11.cloned.1.call-done, bf16[2,4096,1280]{2,1,0:T(8,128)(2,1)} %param.19), kind=kOutput, calls=%fused_computation.46 | convolution fusion | flops 21501050880 | bytes 42991616 | tf_op jit(solution)/shard_map/bsd,df->bsf/dot_general | solution.py:61
  1374.6 28.9 %convolution_convert_fusion = bf16[2,1024,4096]{2,1,0:T(8,128)(2,1)} fusion(bf16[2,1024,1280]{2,1,0:T(8,128)(2,1)} %multiply_convert_fusion, bf16[2,1280,4096]{2,1,0:T(8,128)(2,1)} %param.21), kind=kOutput, calls=%fused_computation.21 | convolution fusion | flops 21483225088 | bytes 32505856 | tf_op jit(solution)/shard_map/bsf,fd->bsd/dot_general | solution.py:64
  1403.6 88.4 %reduce-scatter.11.cloned.1.call-done = bf16[2,128,4096]{2,1,0:T(8,128)(2,1)} async-done(((bf16[2,1024,4096]{2,1,0:T(8,128)(2,1)}), bf16[2,128,4096]{2,1,0:T(8,128)(2,1)}) %reduce-scatter.11.cloned.1.call-update) | async-done | bytes 2097168 | tf_op jit(solution)/shard_map/reduce_scatter | solution.py:65
  1492.0 4.6 fusion.61
  (41 shorter events, 0.2 us)
Async XLA Ops:
  6.5 7.2 copy-start.13
  6.5 455.8 %all-gather.5.cloned.1.call-start = ((), (), s32[]{:S(2)}) async-start(), calls=%async_computation.4 | async-start | bytes 18874368 | tf_op jit(solution)/shard_map/all_gather | solution.py:49
  13.7 660.2 %reduce-scatter.5.cloned.1.call-start = ((), (), s32[]{:S(2)}) async-start(), calls=%async_computation.5 | async-start | bytes 18874368 | tf_op jit(solution)/shard_map/reduce_scatter | solution.py:58
  424.5 31.9 %copy-start.12 = (s32[2,1024]{1,0:T(2,128)S(1)}, s32[2,1024]{1,0:T(2,128)}, u32[]{:S(2)}) copy-start(s32[2,1024]{1,0:T(2,128)} %param.13) | copy-start | bytes 24580
  456.4 34.3 %copy-start.7 = (f32[2,1024]{1,0:T(2,128)}, f32[2,1024]{1,0:T(2,128)S(1)}, u32[]{:S(2)}) copy-start(f32[2,1024]{1,0:T(2,128)S(1)} %compare_select_fusion.5) | copy-start | bytes 24580
  545.1 23.7 %copy-start.6 = (bf16[1,512,4096]{2,1,0:T(8,128)(2,1)S(1)}, bf16[1,512,4096]{2,1,0:T(8,128)(2,1)}, u32[]{:S(2)}) copy-start(bf16[1,512,4096]{2,1,0:T(8,128)(2,1)} %get-tuple-element.7) | copy-start | bytes 12582916
  583.1 0.8 copy-start.11
  583.1 90.8 %copy-start = (bf16[2,128,4096]{2,1,0:T(8,128)(2,1)S(1)}, bf16[2,128,4096]{2,1,0:T(8,128)(2,1)}, u32[]{:S(2)}) copy-start(bf16[2,128,4096]{2,1,0:T(8,128)(2,1)} %param.12) | copy-start | bytes 6291460
  583.2 176.6 %all-gather.7.cloned.1.call-start = ((), (), s32[]{:S(2)}) async-start(), calls=%async_computation.6 | async-start | bytes 18874368 | tf_op jit(solution)/shard_map/all_gather | solution.py:60
  674.0 2.5 copy-start.3
  678.9 255.5 %reduce-scatter.7.cloned.1.call-start = ((), (), s32[]{:S(2)}) async-start(), calls=%async_computation.7 | async-start | bytes 18874368 | tf_op jit(solution)/shard_map/reduce_scatter | solution.py:65
  846.0 93.2 %copy-start.9 = (f32[1,4096]{1,0:T(1,128)S(1)}, f32[1,4096]{1,0:T(1,128)}, u32[]{:S(2)}) copy-start(f32[1,4096]{1,0:T(1,128)} %get-tuple-element.9) | copy-start | bytes 49156
  846.0 176.2 %all-gather.9.cloned.1.call-start = ((), (), s32[]{:S(2)}) async-start(), calls=%async_computation.8 | async-start | bytes 18874368 | tf_op jit(solution)/shard_map/all_gather | solution.py:49
  937.9 1.3 copy-start.1
  941.3 290.4 %reduce-scatter.9.cloned.1.call-start = ((), (), s32[]{:S(2)}) async-start(), calls=%async_computation.9 | async-start | bytes 18874368 | tf_op jit(solution)/shard_map/reduce_scatter | solution.py:58
  1036.0 14.6 copy-start.8
  1105.2 23.7 %copy-start.5 = (bf16[1,512,4096]{2,1,0:T(8,128)(2,1)S(1)}, bf16[1,512,4096]{2,1,0:T(8,128)(2,1)}, u32[]{:S(2)}) copy-start(bf16[1,512,4096]{2,1,0:T(8,128)(2,1)} %get-tuple-element.8) | copy-start | bytes 12582916
  1143.1 88.5 %copy-start.2 = (bf16[2,128,4096]{2,1,0:T(8,128)(2,1)S(1)}, bf16[2,128,4096]{2,1,0:T(8,128)(2,1)}, u32[]{:S(2)}) copy-start(bf16[2,128,4096]{2,1,0:T(8,128)(2,1)} %copy-done.1) | copy-start | bytes 6291460
  1143.1 91.0 %copy-start.10 = (f32[1,4096]{1,0:T(1,128)S(1)}, f32[1,4096]{1,0:T(1,128)}, u32[]{:S(2)}) copy-start(f32[1,4096]{1,0:T(1,128)} %get-tuple-element.12) | copy-start | bytes 49156
  1143.2 174.3 %all-gather.11.cloned.1.call-start = ((), (), s32[]{:S(2)}) async-start(), calls=%async_computation.10 | async-start | bytes 18874368 | tf_op jit(solution)/shard_map/all_gather | solution.py:60
  1231.6 2.5 copy-start.4
  1236.6 255.4 %reduce-scatter.11.cloned.1.call-start = ((), (), s32[]{:S(2)}) async-start(), calls=%async_computation.11 | async-start | bytes 18874368 | tf_op jit(solution)/shard_map/reduce_scatter | solution.py:65
Sparse Core Ops, SparseCore 0:
  13.8 83.9 all-gather.4
  583.3 90.5 reduce-scatter.4
  679.0 80.7 all-gather.6
  846.1 88.2 reduce-scatter.6
  941.4 80.7 all-gather.8
  1143.3 88.2 reduce-scatter.8
  1236.7 80.7 all-gather.10
  1403.7 88.2 reduce-scatter.10
where the time goes:
time: 1510 us; the launch traced here: 1500 us
  waiting for transfers between devices  598 us (40%)
  local copies, waits for them, and re-layouts  452 us (30%)
  matrix products  414 us (27%)
  other arithmetic  26 us (2%)
    unnamed x31, local copies, waits for them, and re-layouts  216 us
    reduce_scatter x2, waiting for transfers between devices, local_fn(): attn_out = lax.psum_scatter(part_out, 'tp', scatter_dimension=1, tiled=True)  178 us
    reduce_scatter x2, waiting for transfers between devices, local_fn(): ffn_out = lax.psum_scatter(part_out, 'tp', scatter_dimension=1, tiled=True)  177 us
    all_gather x2, waiting for transfers between devices, local_fn(): lax.all_gather(rms_norm(mid_resid, norm_mlp[layer_idx]), 'tp', axis=1, ti...  162 us
    reshape x1, local copies, waits for them, and re-layouts, bias_rows(): tiled.reshape(dist_table.shape[0], row_count, 2 * seq_len - 1)  98.6 us
    dot_general x6, matrix products, project(): jnp.einsum('bsd,dn->bsn', gathered, weight_mat, preferred_element_type=jn...  84.1 us
    sub x2, matrix products, local_fn(): jax.nn.softmax(scores + rel_bias + key_bias, axis=-1).astype(jnp.bfloat16)  81.6 us
    all_gather x2, waiting for transfers between devices, local_fn(): lax.all_gather(rms_norm(residual, norm_attn[layer_idx]), 'tp', axis=1, ti...  80.8 us
  transfers between devices with their start and end apart: 8, of which 7 were waited for; matrix products, arithmetic and copies ran while one was open for 30% of the time, Pallas kernels for 0%

commit v1 on v0

v1 whole, which is shorter than its diff:
```python
import functools

import jax
import jax.numpy as jnp
from jax import lax
from jax.experimental import pallas as pl
from jax.experimental.pallas import tpu as pltpu
from jax.sharding import PartitionSpec as P

QT = 128


def rel_bucket(offsets):
    side = jnp.where(offsets > 0, 16, 0)
    distance = jnp.minimum(jnp.abs(offsets), 128)
    limits = 64 * 2 ** jnp.arange(1, 8)
    steps = jnp.sum((distance[..., None] * distance[..., None] >= limits).astype(jnp.int32), axis=-1)
    return side + jnp.where(distance < 8, distance, 8 + steps)


def rms_norm(rows_in, gain_vec):
    rows32 = rows_in.astype(jnp.float32)
    inv_rms = lax.rsqrt(jnp.mean(rows32 * rows32, axis=-1, keepdims=True) + 1e-6)
    return (rows32 * inv_rms * gain_vec).astype(jnp.bfloat16)


def bias_strips(rel_table, seq_len):
    width = 2 * seq_len - QT
    rows = lax.broadcasted_iota(jnp.int32, (QT, width), 0)
    cols = lax.broadcasted_iota(jnp.int32, (QT, width), 1)
    bucket = rel_bucket(cols - rows - (seq_len - QT))
    one_hot = (bucket[None] == lax.broadcasted_iota(jnp.int32, (rel_table.shape[0], QT, width), 0)).astype(jnp.float32)
    return jnp.einsum('bh,brc->hrc', rel_table, one_hot, precision=lax.Precision.HIGHEST)


def attn_kernel(q_ref, k_ref, v_ref, strip_ref, mask_ref, o_ref):
    seq_len = q_ref.shape[0]
    keys = k_ref[...]
    vals = v_ref[...]
    mask = mask_ref[...]
    low = lax.broadcasted_iota(jnp.int32, (QT, 128), 1) < 64

    def tile(i, carry):
        q = q_ref[pl.ds(pl.multiple_of(i * QT, QT), QT), :]
        start = pl.multiple_of(seq_len - QT - i * QT, QT)
        outs = []
        for h in range(2):
            qh = jnp.where(low if h == 0 else jnp.logical_not(low), q, jnp.zeros_like(q))
            s = lax.dot_general(qh, keys, (((1,), (1,)), ((), ())), preferred_element_type=jnp.float32)
            s = s + strip_ref[h, :, pl.ds(start, seq_len)] + mask
            e = jnp.exp(s - jnp.max(s, axis=1, keepdims=True))
            p = (e * (1.0 / jnp.sum(e, axis=1, keepdims=True))).astype(jnp.bfloat16)
            outs.append(jnp.dot(p, vals, preferred_element_type=jnp.float32))
        o_ref[pl.ds(pl.multiple_of(i * QT, QT), QT), :] = jnp.where(low, outs[0], outs[1]).astype(jnp.bfloat16)
        return carry

    lax.fori_loop(0, seq_len // QT, tile, 0)


def attention(q, k, v, strips, mask):
    seq_len, width = q.shape
    pairs = width // 128
    head_block = pl.BlockSpec((seq_len, 128), lambda h: (0, h))
    return pl.pallas_call(
        attn_kernel,
        grid=(pairs,),
        in_specs=[head_block, head_block, head_block,
                  pl.BlockSpec((2, QT, strips.shape[2]), lambda h: (h, 0, 0)),
                  pl.BlockSpec((1, seq_len), lambda h: (0, 0))],
        out_specs=head_block,
        out_shape=jax.ShapeDtypeStruct((seq_len, width), jnp.bfloat16),
        compiler_params=pltpu.CompilerParams(dimension_semantics=('arbitrary',)),
        cost_estimate=pl.CostEstimate(flops=16 * seq_len * seq_len * width, bytes_accessed=8 * seq_len * width,
                                      transcendentals=seq_len * seq_len * 2 * pairs),
        name='attn',
    )(q, k, v, strips, mask)


def solution(mesh):
    group_size = mesh.shape['tp']
    col_spec = P(None, None, 'tp')
    row_spec = P(None, 'tp', None)

    def local_fn(tokens, pad_mask, rel_table, w_query, w_key, w_value, w_out, w_act, w_lin, w_down, norm_attn, norm_mlp):
        batch, seq_loc, model_dim = tokens.shape
        seq_len = seq_loc * group_size
        strips = bias_strips(rel_table, seq_len)
        key_bias = jnp.where(pad_mask == 1, 0.0, -1e9).astype(jnp.float32)

        def mm(a, b):
            return jnp.dot(a, b, preferred_element_type=jnp.float32)

        def entry(resid, gain):
            normed = []
            for s in range(batch):
                if s:
                    resid[s], _ = lax.optimization_barrier((resid[s], normed[s - 1]))
                normed.append(rms_norm(resid[s], gain))
            return [lax.all_gather(n, 'tp', axis=0, tiled=True) for n in normed]

        resid = [tokens[s] for s in range(batch)]
        for layer in range(w_query.shape[0]):
            gathered = entry(resid, norm_attn[layer])
            for s in range(batch):
                h = gathered[s]
                q, k, v = (mm(h, w[layer]).astype(jnp.bfloat16) for w in (w_query, w_key, w_value))
                ctx = attention(q, k, v, strips, key_bias[s:s + 1])
                part = mm(ctx, w_out[layer]).astype(jnp.bfloat16)
                red = lax.psum_scatter(part, 'tp', scatter_dimension=0, tiled=True)
                resid[s] = (resid[s].astype(jnp.float32) + red.astype(jnp.float32)).astype(jnp.bfloat16)
            gathered = entry(resid, norm_mlp[layer])
            for s in range(batch):
                h = gathered[s]
                act = jax.nn.gelu(mm(h, w_act[layer]), approximate=True)
                gated = (act * mm(h, w_lin[layer])).astype(jnp.bfloat16)
                part = mm(gated, w_down[layer]).astype(jnp.bfloat16)
                red = lax.psum_scatter(part, 'tp', scatter_dimension=0, tiled=True)
                resid[s] = (resid[s].astype(jnp.float32) + red.astype(jnp.float32)).astype(jnp.bfloat16)
        return jnp.stack(resid)

    in_specs = (P('dp', 'tp', None), P('dp', None), P(None, 'tp'), col_spec, col_spec, col_spec, row_spec,
                col_spec, col_spec, row_spec, P(None, None), P(None, None))
    return jax.shard_map(local_fn, mesh=mesh, in_specs=in_specs, out_specs=P('dp', 'tp', None), check_vma=False)
```

time: 1510 us -> 918 us (0.61)
  local copies, waits for them, and re-layouts: 452 us -> 12.4 us
  waiting for transfers between devices: 598 us -> 339 us
  Pallas kernels: 0 us -> 162 us
  matrix products: 414 us -> 346 us
    unnamed x31 -> x60, local copies, waits for them, and re-layouts: 216 us -> 3.96 us
    reduce_scatter x4 -> x8, waiting for transfers between devices: 355 us -> 179 us  [local_fn(): red = lax.psum_scatter(part, 'tp', scatter_dimension=0, tiled=True)]
    pallas_call x0 -> x4, Pallas kernels: none -> 162 us  [attention(): pl.pallas_call(attn_kernel, grid=(pairs,), in_specs=[head_block, head_blo...]
    slice x6 -> x3, local copies, waits for them, and re-layouts: 111 us -> 2.68 us  [the longest x1 1.46 us: local_fn(): gathered = entry(resid, norm_attn[layer])]
    reshape x1 -> x0, local copies, waits for them, and re-layouts: 98.6 us -> none  [bias_rows(): tiled.reshape(dist_table.shape[0], row_count, 2 * seq_len - 1)]
    all_gather x4 -> x8, waiting for transfers between devices: 242 us -> 159 us  [entry(): return [lax.all_gather(n, 'tp', axis=0, tiled=True) for n in normed]]
    sub x2 -> x0, matrix products: 81.6 us -> none  [local_fn(): jax.nn.softmax(scores + rel_bias + key_bias, axis=-1).astype(jnp.bfloat16)]
    another operation x1 -> x0, local copies, waits for them, and re-layouts: 21.3 us -> none  [bias_rows(): tiled = jnp.tile(shifted, (1, row_count))[:, :row_count * (2 * seq_len - 1)]]
  transfers between devices with their start and end apart: 8 -> 16, of which waited for: 7 -> 8; matrix products, arithmetic and copies ran while one was open for 30% -> 41% of each run, Pallas kernels for 0% -> 18%
where the time goes in v1:
time: 918 us; the launch traced here: 912 us
  matrix products  346 us (38%)
  waiting for transfers between devices  339 us (37%)
  Pallas kernels  162 us (18%)
  other arithmetic  36.3 us (4%)
  between operations  14.2 us (2%)
  local copies, waits for them, and re-layouts  12.4 us (1%)
    dot_general x28, matrix products, mm(): return jnp.dot(a, b, preferred_element_type=jnp.float32)  336 us
    reduce_scatter x8, waiting for transfers between devices, local_fn(): red = lax.psum_scatter(part, 'tp', scatter_dimension=0, tiled=True)  179 us
    pallas_call x4, Pallas kernels, attention(): pl.pallas_call(attn_kernel, grid=(pairs,), in_specs=[head_block, head_blo...  162 us
    all_gather x8, waiting for transfers between devices, entry(): return [lax.all_gather(n, 'tp', axis=0, tiled=True) for n in normed]  159 us
  transfers between devices with their start and end apart: 16, of which 8 were waited for; matrix products, arithmetic and copies ran while one was open for 41% of the time, Pallas kernels for 18%

profile of v1, /device:TPU:112, one launch (start us, length us, event | category | flops | bytes accessed | tf_op | source)
XLA Modules:
  0.0 911.6 jit_solution(7125000508747616331)
XLA Ops:
  6.6 1.5 fusion.215
  8.0 1.5 fusion.166
  9.5 2.6 fusion.168
  12.3 1.3 slice_bitcast_fusion
  13.9 1.3 fusion.152
  16.5 10.0 %fusion = f32[128,1920,8]{1,2,0:T(8,128)S(1)} fusion(s32[128,1920]{1,0:T(8,128)S(1)} %fusion.208, f32[32,8]{0,1:T(8,128)S(1)} %copy-done), kind=kOutput, calls=%fused_computation.1 | convolution fusion | flops 762839040 | bytes 8848384 | tf_op jit(solution)/shard_map/bh,brc->hrc/dot_general | solution.py:33
  26.5 4.5 copy.16
  31.7 29.0 %all-gather.9.cloned.1.call-done = bf16[1024,4096]{1,0:T(8,128)(2,1)} async-done(((bf16[128,4096]{1,0:T(8,128)(2,1)}), bf16[1024,4096]{1,0:T(8,128)(2,1)}) %all-gather.9.cloned.1.call-update) | async-done | bytes 8388624 | tf_op jit(solution)/shard_map/all_gather | solution.py:99
  60.7 10.2 %fusion.170.q_ref = bf16[1024,512]{1,0:T(8,128)(2,1)} fusion(bf16[1024,4096]{1,0:T(8,128)(2,1)} %all-gather.9.cloned.1.call-done, bf16[2,4096,512]{2,1,0:T(8,128)(2,1)} %param.15), kind=kOutput, calls=%fused_computation.187 | convolution fusion | flops 4295491584 | bytes 13631488 | tf_op jit(solution)/shard_map/dot_general | solution.py:91
  70.9 7.8 fusion.176.k_ref
  78.7 5.5 fusion.182.v_ref
  84.2 49.9 %attn.4 = bf16[1024,512]{1,0:T(8,128)(2,1)} custom-call(bf16[1024,512]{1,0:T(8,128)(2,1)} %fusion.170.q_ref, bf16[1024,512]{1,0:T(8,128)(2,1)} %fusion.176.k_ref, bf16[1024,512]{1,0:T(8,128)(2,1)} %fusion.182.v_ref, f32[8,128,1920]{2,1,0:T(8,128)} %bitcast.174, f32[1,1024]{1,0:T(1,128)} %get-tuple-element.19.mask_ref), custom_call_target="tpu_custom_call" | custom-call | flops 8589934592 | bytes 4194304 | tf_op jit(solution)/shard_map/attn/pallas_call | solution.py:64
  134.1 10.3 %convolution_convert_fusion.3 = bf16[1024,4096]{1,0:T(8,128)(2,1)} fusion(bf16[1024,512]{1,0:T(8,128)(2,1)} %attn.4, bf16[2,512,4096]{2,1,0:T(8,128)(2,1)} %param.18), kind=kOutput, calls=%fused_computation.47 | convolution fusion | flops 4299161600 | bytes 13631488 | tf_op jit(solution)/shard_map/dot_general | solution.py:91
  144.6 10.2 %fusion.173.q_ref = bf16[1024,512]{1,0:T(8,128)(2,1)} fusion(bf16[1024,4096]{1,0:T(8,128)(2,1)} %all-gather.17.cloned.1.call-done, bf16[2,4096,512]{2,1,0:T(8,128)(2,1)} %param.15), kind=kOutput, calls=%fused_computation.188 | convolution fusion | flops 4295491584 | bytes 13631488 | tf_op jit(solution)/shard_map/dot_general | solution.py:91
  154.8 7.8 fusion.179.k_ref
  162.6 5.5 fusion.185.v_ref
  168.0 37.3 %attn.6 = bf16[1024,512]{1,0:T(8,128)(2,1)} custom-call(bf16[1024,512]{1,0:T(8,128)(2,1)} %fusion.173.q_ref, bf16[1024,512]{1,0:T(8,128)(2,1)} %fusion.179.k_ref, bf16[1024,512]{1,0:T(8,128)(2,1)} %fusion.185.v_ref, f32[8,128,1920]{2,1,0:T(8,128)} %bitcast.175, f32[1,1024]{1,0:T(1,128)} %get-tuple-element.20.mask_ref), custom_call_target="tpu_custom_call" | custom-call | flops 8589934592 | bytes 4194304 | tf_op jit(solution)/shard_map/attn/pallas_call | solution.py:64
  205.3 10.3 %convolution_convert_fusion.1 = bf16[1024,4096]{1,0:T(8,128)(2,1)} fusion(bf16[1024,512]{1,0:T(8,128)(2,1)} %attn.6, bf16[2,512,4096]{2,1,0:T(8,128)(2,1)} %param.18), kind=kOutput, calls=%fused_computation.45 | convolution fusion | flops 4299161600 | bytes 13631488 | tf_op jit(solution)/shard_map/dot_general | solution.py:91
  217.3 1.6 fusion.138
  218.9 2.7 fusion.140
  221.8 42.7 %reduce-scatter.17.cloned.1.call-done = bf16[128,4096]{1,0:T(8,128)(2,1)} async-done(((bf16[1024,4096]{1,0:T(8,128)(2,1)}), bf16[128,4096]{1,0:T(8,128)(2,1)}) %reduce-scatter.17.cloned.1.call-update) | async-done | bytes 1048592 | tf_op jit(solution)/shard_map/reduce_scatter | solution.py:109
  264.5 1.6 fusion.153
  267.1 1.3 fusion.156
  268.5 42.6 %all-gather.11.cloned.1.call-done = bf16[1024,4096]{1,0:T(8,128)(2,1)} async-done(((bf16[128,4096]{1,0:T(8,128)(2,1)}), bf16[1024,4096]{1,0:T(8,128)(2,1)}) %all-gather.11.cloned.1.call-update) | async-done | bytes 8388624 | tf_op jit(solution)/shard_map/all_gather | solution.py:99
  311.1 17.5 %fusion.56 = f32[1024,1280]{1,0:T(8,128)S(1)} fusion(bf16[1024,4096]{1,0:T(8,128)(2,1)} %all-gather.11.cloned.1.call-done, bf16[2,4096,1280]{2,1,0:T(8,128)(2,1)} %param.19), kind=kOutput, calls=%fused_computation.59 | convolution fusion | flops 10747904000 | bytes 24117248 | tf_op jit(solution)/shard_map/dot_general | solution.py:91
  328.6 16.3 %multiply_convert_fusion.3 = bf16[1024,1280]{1,0:T(8,128)(2,1)} fusion(f32[1024,1280]{1,0:T(8,128)S(1)} %fusion.56, bf16[1024,4096]{1,0:T(8,128)(2,1)S(1)} %copy-done.18, bf16[2,4096,1280]{2,1,0:T(8,128)(2,1)} %param.20), kind=kOutput, calls=%fused_computation.84 | convolution fusion | flops 10740039680 | bytes 26738688 | tf_op jit(solution)/shard_map/dot_general | solution.py:91
  345.0 16.4 %fusion.38 = bf16[1024,4096]{1,0:T(8,128)(2,1)} fusion(bf16[1024,1280]{1,0:T(8,128)(2,1)} %multiply_convert_fusion.3, bf16[2,1280,4096]{2,1,0:T(8,128)(2,1)} %param.21), kind=kOutput, calls=%fused_computation.48 | convolution fusion | flops 10741612544 | bytes 21495808 | tf_op jit(solution)/shard_map/dot_general | solution.py:91
  361.6 17.3 %fusion.74 = f32[1024,1280]{1,0:T(8,128)S(1)} fusion(bf16[1024,4096]{1,0:T(8,128)(2,1)} %all-gather.19.cloned.1.call-done, bf16[2,4096,1280]{2,1,0:T(8,128)(2,1)} %param.19), kind=kOutput, calls=%fused_computation.73 | convolution fusion | flops 10747904000 | bytes 24117248 | tf_op jit(solution)/shard_map/dot_general | solution.py:91
  378.9 16.3 %multiply_convert_fusion.1 = bf16[1024,1280]{1,0:T(8,128)(2,1)} fusion(f32[1024,1280]{1,0:T(8,128)S(1)} %fusion.74, bf16[1024,4096]{1,0:T(8,128)(2,1)S(1)} %copy-done.19, bf16[2,4096,1280]{2,1,0:T(8,128)(2,1)} %param.20), kind=kOutput, calls=%fused_computation.82 | convolution fusion | flops 10740039680 | bytes 26738688 | tf_op jit(solution)/shard_map/dot_general | solution.py:91
  395.2 16.5 %fusion.41 = bf16[1024,4096]{1,0:T(8,128)(2,1)} fusion(bf16[1024,1280]{1,0:T(8,128)(2,1)} %multiply_convert_fusion.1, bf16[2,1280,4096]{2,1,0:T(8,128)(2,1)} %param.21), kind=kOutput, calls=%fused_computation.49 | convolution fusion | flops 10741612544 | bytes 21495808 | tf_op jit(solution)/shard_map/dot_general | solution.py:91
  412.1 1.2 copy-done.5
  413.3 2.1 fusion.142
  415.5 1.4 fusion.144
  417.0 43.7 %reduce-scatter.19.cloned.1.call-done = bf16[128,4096]{1,0:T(8,128)(2,1)} async-done(((bf16[1024,4096]{1,0:T(8,128)(2,1)}), bf16[128,4096]{1,0:T(8,128)(2,1)}) %reduce-scatter.19.cloned.1.call-update) | async-done | bytes 1048592 | tf_op jit(solution)/shard_map/reduce_scatter | solution.py:117
  460.6 1.8 fusion.157
  462.7 1.3 fusion.160
  464.2 43.2 %all-gather.13.cloned.1.call-done = bf16[1024,4096]{1,0:T(8,128)(2,1)} async-done(((bf16[128,4096]{1,0:T(8,128)(2,1)}), bf16[1024,4096]{1,0:T(8,128)(2,1)}) %all-gather.13.cloned.1.call-update) | async-done | bytes 8388624 | tf_op jit(solution)/shard_map/all_gather | solution.py:99
  507.4 10.2 %fusion.188.q_ref = bf16[1024,512]{1,0:T(8,128)(2,1)} fusion(bf16[1024,4096]{1,0:T(8,128)(2,1)} %all-gather.13.cloned.1.call-done, bf16[2,4096,512]{2,1,0:T(8,128)(2,1)} %param.15), kind=kOutput, calls=%fused_computation.193 | convolution fusion | flops 4295491584 | bytes 13631488 | tf_op jit(solution)/shard_map/dot_general | solution.py:91
  517.6 7.8 fusion.194.k_ref
  525.4 5.5 fusion.200.v_ref
  530.9 37.7 %attn.5 = bf16[1024,512]{1,0:T(8,128)(2,1)} custom-call(bf16[1024,512]{1,0:T(8,128)(2,1)} %fusion.188.q_ref, bf16[1024,512]{1,0:T(8,128)(2,1)} %fusion.194.k_ref, bf16[1024,512]{1,0:T(8,128)(2,1)} %fusion.200.v_ref, f32[8,128,1920]{2,1,0:T(8,128)} %bitcast.176, f32[1,1024]{1,0:T(1,128)} %get-tuple-element.19.mask_ref), custom_call_target="tpu_custom_call" | custom-call | flops 8589934592 | bytes 4194304 | tf_op jit(solution)/shard_map/attn/pallas_call | solution.py:64
  568.6 10.3 %convolution_convert_fusion.2 = bf16[1024,4096]{1,0:T(8,128)(2,1)} fusion(bf16[1024,512]{1,0:T(8,128)(2,1)} %attn.5, bf16[2,512,4096]{2,1,0:T(8,128)(2,1)} %param.18), kind=kOutput, calls=%fused_computation.46 | convolution fusion | flops 4299161600 | bytes 13631488 | tf_op jit(solution)/shard_map/dot_general | solution.py:91
  579.0 10.2 %fusion.191.q_ref = bf16[1024,512]{1,0:T(8,128)(2,1)} fusion(bf16[1024,4096]{1,0:T(8,128)(2,1)} %all-gather.21.cloned.1.call-done, bf16[2,4096,512]{2,1,0:T(8,128)(2,1)} %param.15), kind=kOutput, calls=%fused_computation.194 | convolution fusion | flops 4295491584 | bytes 13631488 | tf_op jit(solution)/shard_map/dot_general | solution.py:91
  589.2 7.8 fusion.197.k_ref
  597.0 5.5 fusion.203.v_ref
  602.5 37.5 %attn.7 = bf16[1024,512]{1,0:T(8,128)(2,1)} custom-call(bf16[1024,512]{1,0:T(8,128)(2,1)} %fusion.191.q_ref, bf16[1024,512]{1,0:T(8,128)(2,1)} %fusion.197.k_ref, bf16[1024,512]{1,0:T(8,128)(2,1)} %fusion.203.v_ref, f32[8,128,1920]{2,1,0:T(8,128)} %bitcast.177, f32[1,1024]{1,0:T(1,128)} %get-tuple-element.20.mask_ref), custom_call_target="tpu_custom_call" | custom-call | flops 8589934592 | bytes 4194304 | tf_op jit(solution)/shard_map/attn/pallas_call | solution.py:64
  639.9 10.3 %convolution_convert_fusion = bf16[1024,4096]{1,0:T(8,128)(2,1)} fusion(bf16[1024,512]{1,0:T(8,128)(2,1)} %attn.7, bf16[2,512,4096]{2,1,0:T(8,128)(2,1)} %param.18), kind=kOutput, calls=%fused_computation.44 | convolution fusion | flops 4299161600 | bytes 13631488 | tf_op jit(solution)/shard_map/dot_general | solution.py:91
  650.4 1.6 fusion.146
  652.1 47.0 %reduce-scatter.21.cloned.1.call-done = bf16[128,4096]{1,0:T(8,128)(2,1)} async-done(((bf16[1024,4096]{1,0:T(8,128)(2,1)}), bf16[128,4096]{1,0:T(8,128)(2,1)}) %reduce-scatter.21.cloned.1.call-update) | async-done | bytes 1048592 | tf_op jit(solution)/shard_map/reduce_scatter | solution.py:109
  699.1 1.6 fusion.161
  700.7 3.1 fusion.148
  704.1 1.3 fusion.164
  706.2 44.5 %all-gather.23.cloned.1.call-done = bf16[1024,4096]{1,0:T(8,128)(2,1)} async-done(((bf16[128,4096]{1,0:T(8,128)(2,1)}), bf16[1024,4096]{1,0:T(8,128)(2,1)}) %all-gather.23.cloned.1.call-update) | async-done | bytes 8388624 | tf_op jit(solution)/shard_map/all_gather | solution.py:99
  750.7 17.3 %fusion.83 = f32[1024,1280]{1,0:T(8,128)S(1)} fusion(bf16[1024,4096]{1,0:T(8,128)(2,1)} %all-gather.23.cloned.1.call-done, bf16[2,4096,1280]{2,1,0:T(8,128)(2,1)} %param.19), kind=kOutput, calls=%fused_computation.80 | convolution fusion | flops 10747904000 | bytes 24117248 | tf_op jit(solution)/shard_map/dot_general | solution.py:91
  768.1 16.3 %multiply_convert_fusion = bf16[1024,1280]{1,0:T(8,128)(2,1)} fusion(f32[1024,1280]{1,0:T(8,128)S(1)} %fusion.83, bf16[1024,4096]{1,0:T(8,128)(2,1)S(1)} %copy-done.21, bf16[2,4096,1280]{2,1,0:T(8,128)(2,1)} %param.20), kind=kOutput, calls=%fused_computation.81 | convolution fusion | flops 10740039680 | bytes 26738688 | tf_op jit(solution)/shard_map/dot_general | solution.py:91
  784.4 16.5 %fusion.47 = bf16[1024,4096]{1,0:T(8,128)(2,1)} fusion(bf16[1024,1280]{1,0:T(8,128)(2,1)} %multiply_convert_fusion, bf16[2,1280,4096]{2,1,0:T(8,128)(2,1)} %param.21), kind=kOutput, calls=%fused_computation.51 | convolution fusion | flops 10741612544 | bytes 21495808 | tf_op jit(solution)/shard_map/dot_general | solution.py:91
  801.1 17.4 %fusion.65 = f32[1024,1280]{1,0:T(8,128)S(1)} fusion(bf16[1024,4096]{1,0:T(8,128)(2,1)} %all-gather.15.cloned.1.call-done, bf16[2,4096,1280]{2,1,0:T(8,128)(2,1)} %param.19), kind=kOutput, calls=%fused_computation.66 | convolution fusion | flops 10747904000 | bytes 24117248 | tf_op jit(solution)/shard_map/dot_general | solution.py:91
  818.5 16.3 %multiply_convert_fusion.2 = bf16[1024,1280]{1,0:T(8,128)(2,1)} fusion(f32[1024,1280]{1,0:T(8,128)S(1)} %fusion.65, bf16[1024,4096]{1,0:T(8,128)(2,1)S(1)} %copy-done.20, bf16[2,4096,1280]{2,1,0:T(8,128)(2,1)} %param.20), kind=kOutput, calls=%fused_computation.83 | convolution fusion | flops 10740039680 | bytes 26738688 | tf_op jit(solution)/shard_map/dot_general | solution.py:91
  834.8 16.4 %fusion.44 = bf16[1024,4096]{1,0:T(8,128)(2,1)} fusion(bf16[1024,1280]{1,0:T(8,128)(2,1)} %multiply_convert_fusion.2, bf16[2,1280,4096]{2,1,0:T(8,128)(2,1)} %param.21), kind=kOutput, calls=%fused_computation.50 | convolution fusion | flops 10741612544 | bytes 21495808 | tf_op jit(solution)/shard_map/dot_general | solution.py:91
  851.4 1.1 copy-done.8
  852.5 2.6 fusion.206
  855.0 45.1 %reduce-scatter.15.cloned.1.call-done = bf16[128,4096]{1,0:T(8,128)(2,1)} async-done(((bf16[1024,4096]{1,0:T(8,128)(2,1)}), bf16[128,4096]{1,0:T(8,128)(2,1)}) %reduce-scatter.15.cloned.1.call-update) | async-done | bytes 1048592 | tf_op jit(solution)/shard_map/reduce_scatter | solution.py:117
  900.1 1.7 fusion.207
  901.9 2.7 pad_maximum_fusion
  (121 shorter events, 7.9 us)
Async XLA Ops:
  6.5 9.9 %copy-start = (f32[32,8]{0,1:T(8,128)S(1)}, f32[32,8]{0,1:T(8,128)}, u32[]{:S(2)}) copy-start(f32[32,8]{0,1:T(8,128)} %param.14) | copy-start | bytes 3076
  6.6 54.1 %all-gather.9.cloned.1.call-start = ((), (), s32[]{:S(2)}) async-start(), calls=%async_computation.8 | async-start | bytes 9437184 | tf_op jit(solution)/shard_map/all_gather | solution.py:99
  12.2 132.4 %all-gather.17.cloned.1.call-start = ((), (), s32[]{:S(2)}) async-start(), calls=%async_computation.16 | async-start | bytes 9437184 | tf_op jit(solution)/shard_map/all_gather | solution.py:99
  15.2 201.8 %reduce-scatter.9.cloned.1.call-start = ((), (), s32[]{:S(2)}) async-start(), calls=%async_computation.9 | async-start | bytes 9437184 | tf_op jit(solution)/shard_map/reduce_scatter | solution.py:109
  26.5 4.5 copy-start.13
  60.6 10.3 %copy-start.15 = (bf16[1024,4096]{1,0:T(8,128)(2,1)S(1)}, bf16[1024,4096]{1,0:T(8,128)(2,1)}, u32[]{:S(2)}) copy-start(bf16[1024,4096]{1,0:T(8,128)(2,1)} %all-gather.9.cloned.1.call-done) | copy-start | bytes 25165828
  60.6 18.1 %slice-start = ((s8[8388608]{0:T(1024)(128)(4,1)}), s8[4194304]{0:T(1024)(128)(4,1)S(1)}, s32[]{:S(2)}) async-start(s8[8388608]{0:T(1024)(128)(4,1)} %bitcast.186), calls=%async_computation.24 | async-start | bytes 8388608
  70.9 7.8 slice-start.1
  144.5 120.0 %reduce-scatter.17.cloned.1.call-start = ((), (), s32[]{:S(2)}) async-start(), calls=%async_computation.17 | async-start | bytes 9437184 | tf_op jit(solution)/shard_map/reduce_scatter | solution.py:109
  144.6 10.2 %copy-start.14 = (bf16[1024,4096]{1,0:T(8,128)(2,1)S(1)}, bf16[1024,4096]{1,0:T(8,128)(2,1)}, u32[]{:S(2)}) copy-start(bf16[1024,4096]{1,0:T(8,128)(2,1)} %all-gather.17.cloned.1.call-done) | copy-start | bytes 25165828
  144.6 18.0 %slice-start.2 = ((s8[8388608]{0:T(1024)(128)(4,1)}), s8[4194304]{0:T(1024)(128)(4,1)S(1)}, s32[]{:S(2)}) async-start(s8[8388608]{0:T(1024)(128)(4,1)} %bitcast.188), calls=%async_computation.26 | async-start | bytes 8388608
  154.8 7.8 slice-start.3
  215.6 0.8 copy-start.12
  215.6 1.6 copy-start.4
  215.7 95.4 %all-gather.11.cloned.1.call-start = ((), (), s32[]{:S(2)}) async-start(), calls=%async_computation.10 | async-start | bytes 9437184 | tf_op jit(solution)/shard_map/all_gather | solution.py:99
  221.7 139.8 %all-gather.19.cloned.1.call-start = ((), (), s32[]{:S(2)}) async-start(), calls=%async_computation.18 | async-start | bytes 9437184 | tf_op jit(solution)/shard_map/all_gather | solution.py:99
  266.1 1.0 copy-start.6
  268.4 143.7 %reduce-scatter.11.cloned.1.call-start = ((), (), s32[]{:S(2)}) async-start(), calls=%async_computation.11 | async-start | bytes 9437184 | tf_op jit(solution)/shard_map/reduce_scatter | solution.py:117
  311.1 17.6 %copy-start.18 = (bf16[1024,4096]{1,0:T(8,128)(2,1)S(1)}, bf16[1024,4096]{1,0:T(8,128)(2,1)}, u32[]{:S(2)}) copy-start(bf16[1024,4096]{1,0:T(8,128)(2,1)} %all-gather.11.cloned.1.call-done) | copy-start | bytes 25165828
  361.5 99.2 %reduce-scatter.19.cloned.1.call-start = ((), (), s32[]{:S(2)}) async-start(), calls=%async_computation.19 | async-start | bytes 9437184 | tf_op jit(solution)/shard_map/reduce_scatter | solution.py:117
  361.6 17.3 %copy-start.19 = (bf16[1024,4096]{1,0:T(8,128)(2,1)S(1)}, bf16[1024,4096]{1,0:T(8,128)(2,1)}, u32[]{:S(2)}) copy-start(bf16[1024,4096]{1,0:T(8,128)(2,1)} %all-gather.19.cloned.1.call-done) | copy-start | bytes 25165828
  411.7 1.6 copy-start.5
  411.7 3.8 copy-start.10
  411.8 95.6 %all-gather.13.cloned.1.call-start = ((), (), s32[]{:S(2)}) async-start(), calls=%async_computation.12 | async-start | bytes 9437184 | tf_op jit(solution)/shard_map/all_gather | solution.py:99
  415.4 285.3 %copy-start.2 = (bf16[128,4096]{1,0:T(8,128)(2,1)}, bf16[128,4096]{1,0:T(8,128)(2,1)S(1)}, u32[]{:S(2)}) copy-start(bf16[128,4096]{1,0:T(8,128)(2,1)S(1)} %get-tuple-element.14) | copy-start | bytes 3145732
  416.9 162.1 %all-gather.21.cloned.1.call-start = ((), (), s32[]{:S(2)}) async-start(), calls=%async_computation.20 | async-start | bytes 9437184 | tf_op jit(solution)/shard_map/all_gather | solution.py:99
  464.1 186.3 %reduce-scatter.13.cloned.1.call-start = ((), (), s32[]{:S(2)}) async-start(), calls=%async_computation.13 | async-start | bytes 9437184 | tf_op jit(solution)/shard_map/reduce_scatter | solution.py:109
  507.4 10.2 %copy-start.17 = (bf16[1024,4096]{1,0:T(8,128)(2,1)S(1)}, bf16[1024,4096]{1,0:T(8,128)(2,1)}, u32[]{:S(2)}) copy-start(bf16[1024,4096]{1,0:T(8,128)(2,1)} %all-gather.13.cloned.1.call-done) | copy-start | bytes 25165828
  507.4 18.0 %slice-start.4 = ((s8[8388608]{0:T(1024)(128)(4,1)}), s8[4194304]{0:T(1024)(128)(4,1)S(1)}, s32[]{:S(2)}) async-start(s8[8388608]{0:T(1024)(128)(4,1)} %bitcast.190), calls=%async_computation.28 | async-start | bytes 8388608
  517.6 7.8 slice-start.5
  578.9 120.2 %reduce-scatter.21.cloned.1.call-start = ((), (), s32[]{:S(2)}) async-start(), calls=%async_computation.21 | async-start | bytes 9437184 | tf_op jit(solution)/shard_map/reduce_scatter | solution.py:109
  579.0 10.2 %copy-start.16 = (bf16[1024,4096]{1,0:T(8,128)(2,1)S(1)}, bf16[1024,4096]{1,0:T(8,128)(2,1)}, u32[]{:S(2)}) copy-start(bf16[1024,4096]{1,0:T(8,128)(2,1)} %all-gather.21.cloned.1.call-done) | copy-start | bytes 25165828
  579.0 18.0 %slice-start.6 = ((s8[8388608]{0:T(1024)(128)(4,1)}), s8[4194304]{0:T(1024)(128)(4,1)S(1)}, s32[]{:S(2)}) async-start(s8[8388608]{0:T(1024)(128)(4,1)} %bitcast.192), calls=%async_computation.30 | async-start | bytes 8388608
  589.2 7.8 slice-start.7
  650.2 50.5 %copy-start.11 = (f32[1,4096]{1,0:T(1,128)S(1)}, f32[1,4096]{1,0:T(1,128)}, u32[]{:S(2)}) copy-start(f32[1,4096]{1,0:T(1,128)} %get-tuple-element.15) | copy-start | bytes 49156
  650.3 100.4 %all-gather.23.cloned.1.call-start = ((), (), s32[]{:S(2)}) async-start(), calls=%async_computation.22 | async-start | bytes 9437184 | tf_op jit(solution)/shard_map/all_gather | solution.py:99
  700.7 67.4 %copy-start.7 = (bf16[128,4096]{1,0:T(8,128)(2,1)}, bf16[128,4096]{1,0:T(8,128)(2,1)S(1)}, u32[]{:S(2)}) copy-start(bf16[128,4096]{1,0:T(8,128)(2,1)S(1)} %fusion.161) | copy-start | bytes 3145732
  705.5 95.6 %all-gather.15.cloned.1.call-start = ((), (), s32[]{:S(2)}) async-start(), calls=%async_computation.14 | async-start | bytes 9437184 | tf_op jit(solution)/shard_map/all_gather | solution.py:99
  706.1 145.2 %reduce-scatter.23.cloned.1.call-start = ((), (), s32[]{:S(2)}) async-start(), calls=%async_computation.23 | async-start | bytes 9437184 | tf_op jit(solution)/shard_map/reduce_scatter | solution.py:117
  750.7 17.4 %copy-start.21 = (bf16[1024,4096]{1,0:T(8,128)(2,1)S(1)}, bf16[1024,4096]{1,0:T(8,128)(2,1)}, u32[]{:S(2)}) copy-start(bf16[1024,4096]{1,0:T(8,128)(2,1)} %all-gather.23.cloned.1.call-done) | copy-start | bytes 25165828
  801.0 99.1 %reduce-scatter.15.cloned.1.call-start = ((), (), s32[]{:S(2)}) async-start(), calls=%async_computation.15 | async-start | bytes 9437184 | tf_op jit(solution)/shard_map/reduce_scatter | solution.py:117
  801.1 17.4 %copy-start.20 = (bf16[1024,4096]{1,0:T(8,128)(2,1)S(1)}, bf16[1024,4096]{1,0:T(8,128)(2,1)}, u32[]{:S(2)}) copy-start(bf16[1024,4096]{1,0:T(8,128)(2,1)} %all-gather.15.cloned.1.call-done) | copy-start | bytes 25165828
  851.2 1.2 copy-start.8
  851.2 48.9 %copy-start.3 = (bf16[128,4096]{1,0:T(8,128)(2,1)S(1)}, bf16[128,4096]{1,0:T(8,128)(2,1)}, u32[]{:S(2)}) copy-start(bf16[128,4096]{1,0:T(8,128)(2,1)} %copy-done.2) | copy-start | bytes 3145732
  851.2 48.9 %copy-start.9 = (bf16[128,4096]{1,0:T(8,128)(2,1)S(1)}, bf16[128,4096]{1,0:T(8,128)(2,1)}, u32[]{:S(2)}) copy-start(bf16[128,4096]{1,0:T(8,128)(2,1)} %reduce-scatter.13.cloned.1.call-done) | copy-start | bytes 3145732
  851.3 53.3 %copy-start.1 = (f32[32,8]{0,1:T(8,128)S(1)}, f32[32,8]{0,1:T(8,128)}, u32[]{:S(2)}) copy-start(f32[32,8]{0,1:T(8,128)} %param.14) | copy-start | bytes 3076
Sparse Core Ops, SparseCore 0:
  12.3 48.2 all-gather.8
  62.2 45.6 all-gather.16
  144.6 48.6 reduce-scatter.8
  215.8 48.6 reduce-scatter.16
  266.0 45.0 all-gather.10
  312.5 45.6 all-gather.18
  361.6 48.6 reduce-scatter.10
  412.5 48.0 reduce-scatter.18
  462.3 45.0 all-gather.12
  508.8 45.6 all-gather.20
  579.0 48.6 reduce-scatter.12
  650.4 48.6 reduce-scatter.20
  705.6 45.0 all-gather.22
  752.2 45.6 all-gather.14
  801.1 48.6 reduce-scatter.22
  851.9 48.1 reduce-scatter.14

commit v2 on v0

v2 whole, which is shorter than its diff:
```python
import functools

import jax
import jax.numpy as jnp
from jax import lax
from jax.experimental import pallas as pl
from jax.experimental.pallas import tpu as pltpu
from jax.sharding import PartitionSpec as P

MESH = pl.DeviceIdType.MESH
CORES = 2
BIAS_BLOCKS = 5
ROWS = 16


def rel_bucket(offsets):
    side = jnp.where(offsets > 0, 16, 0)
    distance = jnp.minimum(jnp.abs(offsets), 128)
    steps = jnp.zeros_like(offsets)
    for octave in range(1, 8):
        steps += (distance * distance >= 64 * 2 ** octave).astype(jnp.int32)
    return side + jnp.where(distance < 8, distance, 8 + steps)


def bias_blocks(table_ref, bias_ref):
    heads, block, _ = bias_ref.shape

    def step(n, carry):
        d, r = lax.rem(n, BIAS_BLOCKS), lax.div(n, BIAS_BLOCKS) * ROWS
        rows = lax.broadcasted_iota(jnp.int32, (ROWS, block), 0) + r
        cols = lax.broadcasted_iota(jnp.int32, (ROWS, block), 1) + (d - BIAS_BLOCKS // 2) * block
        bucket = rel_bucket(cols - rows)
        values = [jnp.full((ROWS, block), table_ref[0, h], jnp.float32) for h in range(heads)]
        for k in range(1, table_ref.shape[0]):
            hit = bucket == k
            values = [jnp.where(hit, table_ref[k, h], values[h]) for h in range(heads)]
        for h in range(heads):
            bias_ref[h, rows_of(r, ROWS), pl.ds(pl.multiple_of(d * block, 128), block)] = values[h]
        return carry

    lax.fori_loop(0, BIAS_BLOCKS * (block // ROWS), step, 0)


def rows_of(start, count):
    return pl.ds(pl.multiple_of(start, ROWS), count)


class Block:
    def __init__(self, chips, layer, x_ref, gain_ref, out_ref, held, pair_in, half_in, full_in, ag_send, ag_recv, rs_send, rs_recv):
        me = lax.axis_index('tp')
        self.chips, self.layer = chips, layer
        self.x_ref, self.gain_ref, self.out_ref, self.held = x_ref, gain_ref, out_ref, held
        self.pair_in, self.half_in, self.full_in = pair_in, half_in, full_in
        self.ag_send, self.ag_recv, self.rs_send, self.rs_recv = ag_send, ag_recv, rs_send, rs_recv
        self.chip, self.core = lax.div(me, CORES), lax.rem(me, CORES)
        self.blk, self.half = x_ref.shape[1], x_ref.shape[1] // 2
        self.right = lax.rem(self.chip + 1, chips)
        self.opp = lax.rem(self.chip + 2, chips)
        self.left = lax.rem(self.chip + 3, chips)
        self.dev_right = self.right * CORES + self.core
        self.dev_left = self.left * CORES + self.core
        self.other = 1 - self.core
        self.partner = self.chip * CORES + self.other

    def barrier(self):
        sem = pltpu.get_barrier_semaphore()
        for dev in (self.dev_left, self.dev_right, self.partner):
            pl.semaphore_signal(sem, inc=1, device_id={'tp': dev}, device_id_type=MESH)
        pl.semaphore_wait(sem, 3)

    def token_rows(self, chip, core, part=None):
        start = (chip * CORES + core) * self.blk
        if part is None:
            return rows_of(start, self.blk)
        return rows_of(start + part * self.half, self.half)

    def norm(self, s):
        own = (self.chip * CORES + self.core) * self.blk

        def step(i, carry):
            x = self.x_ref[s, rows_of(i * ROWS, ROWS), :].astype(jnp.float32)
            inv = lax.rsqrt(jnp.mean(x * x, axis=-1, keepdims=True) + 1e-6)
            self.held[s, rows_of(own + i * ROWS, ROWS), :] = (x * inv * self.gain_ref[self.layer:self.layer + 1, :]).astype(jnp.bfloat16)
            return carry

        lax.fori_loop(0, self.blk // ROWS, step, 0)

    def _ag(self, s, k, rows, dev):
        ref = self.held.at[s, rows]
        return pltpu.make_async_remote_copy(src_ref=ref, dst_ref=ref, send_sem=self.ag_send.at[s, k],
                                            recv_sem=self.ag_recv.at[s, k], device_id={'tp': dev}, device_id_type=MESH)

    def ag_copy(self, s, k):
        c = self.core
        rows = (lambda: self.token_rows(self.chip, c, 0), lambda: self.token_rows(self.chip, c, 1),
                lambda: self.token_rows(self.chip, c, 1), lambda: self.token_rows(self.chip, c, 0),
                lambda: self.token_rows(self.left, c, 0), lambda: self.token_rows(self.right, c, 1),
                lambda: self.token_rows(self.chip, c), lambda: self.token_rows(self.left, c),
                lambda: self.token_rows(self.right, c), lambda: self.token_rows(self.opp, c))[k]()
        dev = (self.dev_right, self.dev_right, self.dev_left, self.dev_left, self.dev_right, self.dev_left,
               self.partner, self.partner, self.partner, self.partner)[k]
        return self._ag(s, k, rows, dev)

    def ag_wait(self, s, *which):
        c, o = self.core, self.other
        rows = [self.token_rows(self.left, c, 0), self.token_rows(self.left, c, 1), self.token_rows(self.right, c, 1),
                self.token_rows(self.right, c, 0), self.token_rows(self.opp, c, 0), self.token_rows(self.opp, c, 1),
                self.token_rows(self.chip, o), self.token_rows(self.left, o), self.token_rows(self.right, o),
                self.token_rows(self.opp, o)]
        for k in which:
            self._ag(s, k, rows[k], self.partner).wait_recv()

    def ag_start(self, s):
        for k in (0, 2, 1, 3):
            self.ag_copy(s, k).start()

    def ag_forward(self, s):
        self.ag_wait(s, 0)
        self.ag_copy(s, 4).start()
        self.ag_wait(s, 2)
        self.ag_copy(s, 5).start()

    def ag_share(self, s):
        self.ag_wait(s, 1)
        self.ag_copy(s, 7).start()
        self.ag_wait(s, 3)
        self.ag_copy(s, 8).start()

    def ag_share_opp(self, s):
        self.ag_wait(s, 4, 5)
        self.ag_copy(s, 9).start()

    def ag_drain(self, s):
        for k in range(10):
            self.ag_copy(s, k).wait_send()

    def _rs(self, s, k, rows, dst, dev):
        return pltpu.make_async_remote_copy(src_ref=self.held.at[s, rows], dst_ref=dst, send_sem=self.rs_send.at[s, k],
                                            recv_sem=self.rs_recv.at[s, k], device_id={'tp': dev}, device_id_type=MESH)

    def rs_copy(self, s, k):
        c, o, h = self.core, self.other, self.half
        lo, hi = pl.ds(0, h), pl.ds(h, h)
        if k < 4:
            chip = (self.opp, self.right, self.left, self.chip)[k]
            return self._rs(s, k, self.token_rows(chip, o), self.pair_in.at[s, k], self.partner)
        chip, part, dst = ((self.opp, 0, self.half_in.at[s, 0]), (self.opp, 1, self.half_in.at[s, 1]),
                           (self.right, 1, self.full_in.at[s, 0, hi]), (self.left, 0, self.full_in.at[s, 1, lo]),
                           (self.right, 0, self.full_in.at[s, 0, lo]), (self.left, 1, self.full_in.at[s, 1, hi]))[k - 4]
        return self._rs(s, k, self.token_rows(chip, c, part), dst, self.dev_left if k % 2 else self.dev_right)

    def rs_pair(self, s, *which):
        for k in which:
            self.rs_copy(s, k).start()

    def _add(self, s, start, count, other):
        def step(i, carry):
            at = rows_of(start + i * ROWS, ROWS)
            total = self.held[s, at, :].astype(jnp.float32) + other(rows_of(i * ROWS, ROWS)).astype(jnp.float32)
            self.held[s, at, :] = total.astype(jnp.bfloat16)
            return carry

        lax.fori_loop(0, count // ROWS, step, 0)

    def rs_first(self, s, *which):
        for k in which:
            chip, then = ((self.opp, (4, 5)), (self.right, (6,)), (self.left, (7,)), (self.chip, ()))[k]
            self.rs_copy(s, k).wait_recv()
            self._add(s, (chip * CORES + self.core) * self.blk, self.blk, lambda at: self.pair_in[s, k, at, :])
            for j in then:
                self.rs_copy(s, j).start()

    def rs_second(self, s):
        for k, chip, part in ((4, self.right, 0), (5, self.left, 1)):
            self.rs_copy(s, k).wait_recv()
            start = (chip * CORES + self.core) * self.blk + part * self.half
            self._add(s, start, self.half, lambda at: self.half_in[s, part, at, :])
            self.rs_copy(s, k + 4).start()

    def rs_last(self, s):
        for k in (6, 7, 8, 9):
            self.rs_copy(s, k).wait_recv()
        own = (self.chip * CORES + self.core) * self.blk

        def step(i, carry):
            at = rows_of(i * ROWS, ROWS)
            total = self.held[s, rows_of(own + i * ROWS, ROWS), :].astype(jnp.float32)
            total = total + self.full_in[s, 0, at, :].astype(jnp.float32) + self.full_in[s, 1, at, :].astype(jnp.float32)
            self.out_ref[s, at, :] = (self.x_ref[s, at, :].astype(jnp.float32) + total).astype(jnp.bfloat16)
            return carry

        lax.fori_loop(0, self.blk // ROWS, step, 0)

    def rs_drain(self, s):
        for k in range(10):
            self.rs_copy(s, k).wait_send()


def run_block(b, first, middle, second, prepare, early, restore):
    def tail(s, between):
        second(s, (b.opp, b.right), 0)
        second(s, (b.opp, b.right), 1)
        b.rs_pair(s, 0, 1)
        between()
        second(s, (b.left, b.chip), 0)
        b.rs_first(s, 0, 1)
        second(s, (b.left, b.chip), 1)
        b.rs_pair(s, 2, 3)

    b.barrier()
    prepare()
    b.norm(0)
    b.ag_start(0)
    b.ag_copy(0, 6).start()
    b.norm(1)
    b.ag_copy(1, 6).start()
    early()
    b.ag_wait(0, 6)
    first(0, b.chip)
    b.ag_wait(1, 6)
    first(1, b.chip, True)
    b.ag_forward(0)
    b.ag_start(1)
    b.ag_share(0)
    b.ag_wait(0, 7)
    first(0, b.left)
    b.ag_wait(0, 8)
    first(0, b.right)
    b.ag_share_opp(0)
    b.ag_wait(0, 9)
    first(0, b.opp)
    middle(0, lambda: b.ag_forward(1))
    b.ag_drain(0)
    tail(0, lambda: None)
    b.ag_share(1)
    b.rs_first(0, 2, 3)
    restore()
    b.ag_share_opp(1)
    b.ag_wait(1, 7)
    first(1, b.left)
    b.ag_wait(1, 8)
    first(1, b.right)
    b.ag_wait(1, 9)
    first(1, b.opp)
    middle(1, lambda: b.rs_second(0))
    b.ag_drain(1)
    tail(1, lambda: None)
    b.rs_first(1, 2, 3)
    b.rs_last(0)
    b.rs_drain(0)
    b.rs_second(1)
    b.rs_last(1)
    b.rs_drain(1)


def attn_kernel(chips, layer, x_ref, gain_ref, table_ref, pad_ref, wq_ref, wk_ref, wv_ref, wo_ref, out_ref,
                held, pair_in, half_in, full_in, w_in, w_back, proj, ctx, bias_ref, mask_ref, score_a, score_b, probs_ref, w_sem, ag_send, ag_recv, rs_send, rs_recv):
    b = Block(chips, layer, x_ref, gain_ref, out_ref, held, pair_in, half_in, full_in, ag_send, ag_recv, rs_send, rs_recv)
    seq_len, model_dim = held.shape[1], held.shape[2]
    width = proj.shape[2]
    blk = b.blk
    chip_rows = CORES * blk
    blocks = seq_len // blk
    score_refs = (score_a, score_b)
    loads = [pltpu.make_async_copy(w.at[layer], w_in.at[j], w_sem.at[j]) for j, w in enumerate((wq_ref, wk_ref, wv_ref))]
    load_out = pltpu.make_async_copy(wo_ref.at[layer], w_back, w_sem.at[3])

    def prepare():
        for load in loads + [load_out]:
            load.start()

    started = []

    def early():
        bias_blocks(table_ref, bias_ref)
        mask_ref[...] = jnp.where(pad_ref[...] == 1, 0.0, -1e9).astype(jnp.float32)

    def restore():
        def step(j, carry):
            proj[j, rows_of(b.chip * chip_rows, chip_rows), :] = proj[j, seq_len:, :]
            return carry

        lax.fori_loop(0, 3, step, 0)

    def first(s, chip, aside=False):
        if not started:
            started.append(0)
            for load in loads:
                load.wait()
        rows = rows_of(chip * chip_rows, chip_rows)
        to = pl.ds(seq_len, chip_rows) if aside else rows

        def step(j, carry):
            product = jnp.dot(held[s, rows, :], w_in[j], preferred_element_type=jnp.float32)
            proj[j, to, :] = product.astype(jnp.bfloat16)
            return carry

        lax.fori_loop(0, 3, step, 0)

    low = lax.broadcasted_iota(jnp.int32, (chip_rows, 128), 1) < 64

    group = 32

    def scores_of(n, slot):
        pair, i = lax.div(n, chips), lax.rem(n, chips)
        cols = pl.ds(pl.multiple_of(pair * 128, 128), 128)
        q = proj[0, rows_of(i * chip_rows, chip_rows), cols]
        zero = jnp.zeros_like(q)
        both = jnp.concatenate([jnp.where(low, q, zero), jnp.where(low, zero, q)], axis=0)
        score_refs[slot][...] = lax.dot_general(both, proj[1, :seq_len, cols], (((1,), (1,)), ((), ())),
                                                preferred_element_type=jnp.float32)

    def attend(s, n, slot):
        pair, i = lax.div(n, chips), lax.rem(n, chips)
        cols = pl.ds(pl.multiple_of(pair * 128, 128), 128)
        mask = mask_ref[pl.ds(s, 1), :]
        for part in range(2 * CORES):
            h, sub = part // CORES, part % CORES
            at = [(jnp.clip(j - i * CORES - sub, -(BIAS_BLOCKS // 2), BIAS_BLOCKS // 2) + BIAS_BLOCKS // 2) * blk
                  for j in range(blocks)]
            for r in range(0, blk, group):
                pieces = [score_refs[slot][part * blk + r:part * blk + r + group, j * blk:(j + 1) * blk]
                          + bias_ref[pair * 2 + h, r:r + group, pl.ds(pl.multiple_of(at[j], 128), blk)]
                          + mask[:, j * blk:(j + 1) * blk] for j in range(blocks)]
                full = jnp.concatenate(pieces, axis=1)
                e = jnp.exp(full - jnp.max(full, axis=1, keepdims=True))
                probs_ref[part * blk + r:part * blk + r + group, :] = (
                    e * (1.0 / jnp.sum(e, axis=1, keepdims=True))).astype(jnp.bfloat16)
        outs = jnp.dot(probs_ref[...], proj[2, :seq_len, cols], preferred_element_type=jnp.float32)
        ctx[rows_of(i * chip_rows, chip_rows), cols] = jnp.where(low, outs[:chip_rows], outs[chip_rows:]).astype(jnp.bfloat16)

    def middle(s, hook):
        count = (width // 128) * chips
        scores_of(0, 0)

        def step(m, carry):
            n = 2 * m
            scores_of(n + 1, 1)
            attend(s, n, 0)
            scores_of(jnp.minimum(n + 2, count - 1), 0)
            attend(s, n + 1, 1)
            return carry

        lax.fori_loop(0, count // 4, step, 0)
        hook()
        lax.fori_loop(count // 4, count // 2, step, 0)
        if s == 0:
            load_out.wait()

    tile = 512

    def second(s, which, part):
        tiles = model_dim // tile

        def step(n, carry):
            cols = pl.ds(pl.multiple_of(n * tile, tile), tile)
            for chip in which:
                rows = rows_of(chip * chip_rows, chip_rows)
                held[s, rows, cols] = jnp.dot(ctx[rows, :], w_back[:, cols], preferred_element_type=jnp.float32).astype(jnp.bfloat16)
            return carry

        lax.fori_loop(part * tiles // 2, (part + 1) * tiles // 2, step, 0)

    run_block(b, first, middle, second, prepare, early, restore)


def ffn_kernel(chips, layer, x_ref, gain_ref, wa_ref, wl_ref, wd_ref, out_ref,
               held, pair_in, half_in, full_in, w_in, w_back, gated, w_sem, d_sem, ag_send, ag_recv, rs_send, rs_recv):
    b = Block(chips, layer, x_ref, gain_ref, out_ref, held, pair_in, half_in, full_in, ag_send, ag_recv, rs_send, rs_recv)
    model_dim = held.shape[2]
    seq_len, width = held.shape[1], gated.shape[1]
    blk = b.blk
    chip_rows = CORES * blk
    tile_in, tile_out = 256, w_back.shape[2]
    loads = [pltpu.make_async_copy(w.at[layer, :, pl.ds(n * tile_in, tile_in)],
                                   w_in.at[n, :, pl.ds(half * tile_in, tile_in)], w_sem.at[2 * n + half])
             for n in range(width // tile_in) for half, w in enumerate((wa_ref, wl_ref))]

    def prepare():
        for load in loads:
            load.start()

    started = []

    def restore():
        gated[rows_of(b.chip * chip_rows, chip_rows), :] = gated[seq_len:, :]

    def first(s, chip, aside=False):
        if not started:
            started.append(0)
            for load in loads:
                load.wait()
        rows = rows_of(chip * chip_rows, chip_rows)
        to = pl.ds(seq_len, chip_rows) if aside else rows

        def step(n, carry):
            cols = pl.ds(pl.multiple_of(n * tile_in, tile_in), tile_in)
            both = jnp.dot(held[s, rows, :], w_in[n], preferred_element_type=jnp.float32)
            act, lin = both[:, :tile_in], both[:, tile_in:]
            gated[to, cols] = (jax.nn.gelu(act, approximate=True) * lin).astype(jnp.bfloat16)
            return carry

        lax.fori_loop(0, width // tile_in, step, 0)

    tiles = model_dim // tile_out

    def load_back(n):
        cols = pl.ds(pl.multiple_of(n * tile_out, tile_out), tile_out)
        slot = lax.rem(n, 2)
        return pltpu.make_async_copy(wd_ref.at[layer, :, cols], w_back.at[slot], d_sem.at[slot])

    def second(s, which, part):
        if part == 0:
            load_back(0).start()

        def step(n, carry):
            @pl.when(n + 1 < tiles)
            def _():
                load_back(n + 1).start()

            load_back(n).wait()
            cols = pl.ds(pl.multiple_of(n * tile_out, tile_out), tile_out)
            for chip in which:
                rows = rows_of(chip * chip_rows, chip_rows)
                product = jnp.dot(gated[rows, :], w_back[lax.rem(n, 2)], preferred_element_type=jnp.float32)
                held[s, rows, cols] = product.astype(jnp.bfloat16)
            return carry

        lax.fori_loop(part * tiles // 2, (part + 1) * tiles // 2, step, 0)

    run_block(b, first, lambda s, hook: hook(), second, prepare, lambda: None, restore)


def comm_scratch(batch, seq_len, blk, dim):
    chips = seq_len // (CORES * blk)
    return [pltpu.VMEM((batch, seq_len, dim), jnp.bfloat16), pltpu.VMEM((batch, chips, blk, dim), jnp.bfloat16),
            pltpu.VMEM((batch, 2, blk // 2, dim), jnp.bfloat16), pltpu.VMEM((batch, 2, blk, dim), jnp.bfloat16)]


def comm_sems(batch):
    return [pltpu.SemaphoreType.DMA((batch, 10))] * 4


def call_block(kernel, name, cid, x, operands, extra, sems, flops, placed):
    batch, blk, dim = x.shape
    spaces = (pl.BlockSpec(memory_space=pl.ANY), pl.BlockSpec(memory_space=pltpu.VMEM), pl.BlockSpec(memory_space=pltpu.SMEM))
    seq_len = extra[0]
    return pl.pallas_call(
        kernel,
        out_shape=jax.ShapeDtypeStruct(x.shape, x.dtype),
        in_specs=[spaces[1]] + [spaces[where] for where in placed],
        out_specs=spaces[1],
        scratch_shapes=comm_scratch(batch, seq_len, blk, dim) + extra[1] + sems + comm_sems(batch),
        compiler_params=pltpu.CompilerParams(collective_id=cid, has_side_effects=True, vmem_limit_bytes=67_000_000),
        cost_estimate=pl.CostEstimate(flops=flops, bytes_accessed=0, transcendentals=0),
        name=name,
    )(x, *operands)


def solution(mesh):
    group_size = mesh.shape['tp']
    chips = group_size // CORES
    col_spec = P(None, None, 'tp')
    row_spec = P(None, 'tp', None)

    def local_fn(tokens, pad_mask, rel_table, w_query, w_key, w_value, w_out, w_act, w_lin, w_down, norm_attn, norm_mlp):
        batch, blk, dim = tokens.shape
        seq_len = blk * group_size
        width, ff = w_query.shape[2], w_act.shape[2]
        x = tokens
        for layer in range(w_query.shape[0]):
            x = call_block(
                functools.partial(attn_kernel, chips, layer), 'attn_block', 2 * layer, x,
                (norm_attn, rel_table, pad_mask, w_query, w_key, w_value, w_out),
                (seq_len, [pltpu.VMEM((3, dim, width), jnp.bfloat16), pltpu.VMEM((width, dim), jnp.bfloat16),
                           pltpu.VMEM((3, seq_len + CORES * blk, width), jnp.bfloat16), pltpu.VMEM((seq_len, width), jnp.bfloat16),
                           pltpu.VMEM((rel_table.shape[1], blk, BIAS_BLOCKS * blk), jnp.float32), pltpu.VMEM((batch, seq_len), jnp.float32),
                           pltpu.VMEM((2 * CORES * blk, seq_len), jnp.float32), pltpu.VMEM((2 * CORES * blk, seq_len), jnp.float32),
                           pltpu.VMEM((2 * CORES * blk, seq_len), jnp.bfloat16)]),
                [pltpu.SemaphoreType.DMA((4,))], 8 * batch * seq_len * dim * width, (1, 2, 1, 0, 0, 0, 0))
            x = call_block(
                functools.partial(ffn_kernel, chips, layer), 'ffn_block', 2 * layer + 1, x,
                (norm_mlp, w_act, w_lin, w_down),
                (seq_len, [pltpu.VMEM((ff // 256, dim, 512), jnp.bfloat16),
                           pltpu.VMEM((2, ff, 512), jnp.bfloat16), pltpu.VMEM((seq_len + CORES * blk, ff), jnp.bfloat16)]),
                [pltpu.SemaphoreType.DMA((2 * (ff // 256),)), pltpu.SemaphoreType.DMA((2,))], 6 * batch * seq_len * dim * ff, (1, 0, 0, 0))
        return x

    in_specs = (P('dp', 'tp', None), P('dp', None), P(None, 'tp'), col_spec, col_spec, col_spec, row_spec,
                col_spec, col_spec, row_spec, P(None, None), P(None, None))
    return jax.shard_map(local_fn, mesh=mesh, in_specs=in_specs, out_specs=P('dp', 'tp', None), check_vma=False)
```

time: 1510 us -> 630 us (0.42)
  Pallas kernels: 0 us -> 615 us
  waiting for transfers between devices: 598 us -> 0 us
  local copies, waits for them, and re-layouts: 452 us -> 4.49 us
  matrix products: 414 us -> 0 us
  other arithmetic: 26 us -> 0 us
    pallas_call x0 -> x4, Pallas kernels: none -> 615 us  [call_block(): pl.pallas_call(kernel, out_shape=jax.ShapeDtypeStruct(x.shape, x.dtype),...]
    reduce_scatter x4 -> x0, waiting for transfers between devices: 355 us -> none  [the longest x2 178 us: local_fn(): attn_out = lax.psum_scatter(part_out, 'tp', scatter_dimension=1, tiled=True)]
    dot_general x16 -> x0, matrix products: 332 us -> none  [the longest x6 84.1 us: project(): jnp.einsum('bsd,dn->bsn', gathered, weight_mat, preferred_element_type=jn...]
    all_gather x4 -> x0, waiting for transfers between devices: 242 us -> none  [the longest x2 162 us: local_fn(): lax.all_gather(rms_norm(mid_resid, norm_mlp[layer_idx]), 'tp', axis=1, ti...]
    unnamed x31 -> x2, local copies, waits for them, and re-layouts: 216 us -> 4.49 us
    slice x6 -> x0, local copies, waits for them, and re-layouts: 111 us -> none  [the longest x2 58.3 us: bias_rows(): tiled.reshape(dist_table.shape[0], row_count, 2 * seq_len - 1)]
    reshape x1 -> x0, local copies, waits for them, and re-layouts: 98.6 us -> none  [bias_rows(): tiled.reshape(dist_table.shape[0], row_count, 2 * seq_len - 1)]
    sub x2 -> x0, matrix products: 81.6 us -> none  [local_fn(): jax.nn.softmax(scores + rel_bias + key_bias, axis=-1).astype(jnp.bfloat16)]
  transfers between devices with their start and end apart: 8 -> 0, of which waited for: 7 -> 0; matrix products, arithmetic and copies ran while one was open for 30% -> 0% of each run, Pallas kernels for 0% -> 0%
where the time goes in v2:
time: 630 us; the launch traced here: 619 us
  Pallas kernels  615 us (98%)
    pallas_call x4, Pallas kernels, call_block(): pl.pallas_call(kernel, out_shape=jax.ShapeDtypeStruct(x.shape, x.dtype),...  615 us

profile of v2, /device:TPU:112, one launch (start us, length us, event | category | flops | bytes accessed | tf_op | source)
XLA Modules:
  0.0 619.5 jit_solution(2903590750251427013)
XLA Ops:
  0.0 1.4 copy.13.table_ref
  1.4 157.3 %attn_block.2.x_ref = bf16[2,128,4096]{2,1,0:T(8,128)(2,1)} custom-call(bf16[2,128,4096]{2,1,0:T(8,128)(2,1)} %x_ref.1, f32[2,4096]{1,0:T(2,128)} %gain_ref.6, f32[32,8]{1,0:T(8,128)} %copy.13.table_ref, s32[2,1024]{1,0:T(2,128)} %pad_ref.3, bf16[2,4096,512]{2,1,0:T(8,128)(2,1)} %wq_ref.3, bf16[2,4096,512]{2,1,0:T(8,128)(2,1)} %wk_ref.3, ...), custom_call_target="tpu_custom_call" | custom-call | flops 34359738368 | tf_op jit(solution)/shard_map/attn_block/pallas_call | solution.py:448
  158.6 150.5 %ffn_block.2.x_ref = bf16[2,128,4096]{2,1,0:T(8,128)(2,1)} custom-call(bf16[2,128,4096]{2,1,0:T(8,128)(2,1)} %attn_block.2.x_ref, f32[2,4096]{1,0:T(2,128)} %gain_ref.7, bf16[2,4096,1280]{2,1,0:T(8,128)(2,1)} %wa_ref.3, bf16[2,4096,1280]{2,1,0:T(8,128)(2,1)} %wl_ref.3, bf16[2,1280,4096]{2,1,0:T(8,128)(2,1)} %wd_ref.3), custom_call_target="tpu_custom_call" | custom-call | flops 64424509440 | tf_op jit(solution)/shard_map/ffn_block/pallas_call | solution.py:448
  309.1 156.7 %attn_block.3.x_ref = bf16[2,128,4096]{2,1,0:T(8,128)(2,1)} custom-call(bf16[2,128,4096]{2,1,0:T(8,128)(2,1)} %ffn_block.2.x_ref, f32[2,4096]{1,0:T(2,128)} %gain_ref.6, f32[32,8]{1,0:T(8,128)} %copy.13.table_ref, s32[2,1024]{1,0:T(2,128)} %pad_ref.3, bf16[2,4096,512]{2,1,0:T(8,128)(2,1)} %wq_ref.3, bf16[2,4096,512]{2,1,0:T(8,128)(2,1)} %wk_ref.3, ...), custom_call_target="tpu_custom_call" | custom-call | flops 34359738368 | tf_op jit(solution)/shard_map/attn_block/pallas_call | solution.py:448
  465.8 150.1 %ffn_block.3 = bf16[2,128,4096]{2,1,0:T(8,128)(2,1)} custom-call(bf16[2,128,4096]{2,1,0:T(8,128)(2,1)} %attn_block.3.x_ref, f32[2,4096]{1,0:T(2,128)} %gain_ref.7, bf16[2,4096,1280]{2,1,0:T(8,128)(2,1)} %wa_ref.3, bf16[2,4096,1280]{2,1,0:T(8,128)(2,1)} %wl_ref.3, bf16[2,1280,4096]{2,1,0:T(8,128)(2,1)} %wd_ref.3), custom_call_target="tpu_custom_call" | custom-call | flops 64424509440 | tf_op jit(solution)/shard_map/ffn_block/pallas_call | solution.py:448
  615.9 3.1 copy.16
